TPU v7x, 32 devices: a whole 2x2x4 slice. The times are simulated.
32 devices in a mesh: dp: 8 (over y, x, core), tensor: 4 (over z).
Axes of the slice: x: 2, y: 2, z: 4, core: 2. Of those that a mesh axis runs over, the one named last changes fastest.
Arguments:
- grad_out: bfloat16 [2048, 4096], P('dp'), may hold values from -6 to 6
- down_weight: bfloat16 [14336, 4096], P('tensor'), may hold values from -0.046875 to 0.046875
- gate_pre: bfloat16 [2048, 14336], P('dp', 'tensor'), may hold values from -8 to 8
- up_pre: bfloat16 [2048, 14336], P('dp', 'tensor'), may hold values from -6 to 6
Outputs:
- factor: float32 [14336, 14336], P('dp', 'tensor')
- grad_up: bfloat16 [2048, 14336], P('dp', 'tensor')
All inputs are finite; a program needn't handle non-finite values.
Results may differ from a plain program's by a relative error of at most 0.0046.
Values may be sent and summed in bfloat16 or wider, within the bound.
A program may use at most 128 MiB of HBM per device.

v0:
```python
import jax
import jax.numpy as jnp
from jax import lax
from jax.sharding import PartitionSpec as P


def local(grad_out, down_weight, gate_pre, up_pre):
    hidden_grad = lax.dot_general(
        grad_out, down_weight, (((1,), (1,)), ((), ())), preferred_element_type=jnp.float32
    )
    gate_value = gate_pre.astype(jnp.float32)
    sigmoid_gate = jax.nn.sigmoid(gate_value)
    silu_slope = sigmoid_gate * (1.0 + gate_value * (1.0 - sigmoid_gate))
    grad_gate = (hidden_grad * up_pre.astype(jnp.float32) * silu_slope).astype(jnp.bfloat16)
    grad_up = (hidden_grad * gate_value * sigmoid_gate).astype(jnp.bfloat16)
    replicas = lax.axis_size("dp")
    token_total = grad_gate.shape[0] * replicas
    all_columns_grad = lax.all_gather(grad_gate, "tensor", axis=1, tiled=True)
    row_block = lax.all_to_all(all_columns_grad, "dp", split_axis=1, concat_axis=0, tiled=True)
    factor_tile = lax.dot_general(
        row_block,
        lax.all_gather(grad_gate, "dp", axis=0, tiled=True),
        (((0,), (0,)), ((), ())),
        preferred_element_type=jnp.float32,
    )
    factor = factor_tile / jnp.float32(token_total)
    return (factor, grad_up)


def solution(mesh):
    placed = (P("dp", None), P("tensor", None), P("dp", "tensor"), P("dp", "tensor"))
    return jax.shard_map(
        local,
        mesh=mesh,
        in_specs=placed,
        out_specs=(P("dp", "tensor"), P("dp", "tensor")),
        check_vma=False,
    )
```

profile of v0, /device:TPU:6, one launch (start us, length us, event | category | flops | bytes accessed | tf_op | source)
XLA Modules:
  0.0 349.3 jit_solution(13841127326262000508)
XLA Ops:
  7.2 0.0 copy-start
  7.2 0.0 all-gather.3.cloned.1.call-start
  7.2 1.5 copy-done
  8.8 16.8 %fusion.8 = (bf16[256,3584]{1,0:T(8,128)(2,1)}, bf16[256,3584]{1,0:T(8,128)(2,1)}) fusion(bf16[256,3584]{1,0:T(8,128)(2,1)} %param.6, bf16[256,3584]{1,0:T(8,128)(2,1)} %param.7, bf16[256,4096]{1,0:T(8,128)(2,1)S(1)} %copy-done, bf16[3584,4096]{1,0:T(8,128)(2,1)} %param.5), kind=kOutput, calls=%fused_computation.13 | convolution fusion | flops 7529955328 | bytes 38797312 | tf_op jit(solution)/shard_map/dot_general | solution.py:8
  25.6 0.0 all-gather.3.cloned.1.call-update
  25.6 0.0 all-gather.5.cloned.1.call-start
  25.7 0.7 all-gather.5.cloned.1.call-update
  26.4 133.1 %all-gather.3.cloned.1.call-done = bf16[256,14336]{1,0:T(8,128)(2,1)} async-done(((bf16[256,3584]{1,0:T(8,128)(2,1)}), bf16[256,14336]{1,0:T(8,128)(2,1)}) %all-gather.3.cloned.1.call-update) | async-done | bytes 7340048 | tf_op jit(solution)/shard_map/all_gather | solution.py:18
  159.4 3.6 %copy.9 = bf16[32,8,8,1792]{3,2,0,1:T(8,128)(2,1)S(1)} copy(bf16[32,8,8,1792]{3,2,1,0:T(8,128)(2,1)} %bitcast.12) | data formatting | bytes 14680064 | tf_op jit(solution)/shard_map/all_to_all | solution.py:19
  163.0 133.4 %all_to_all.19 = bf16[256,8,1792]{2,0,1:T(8,128)(2,1)} all-to-all(bf16[256,8,1792]{2,0,1:T(8,128)(2,1)S(1)} %bitcast.11), channel_id=1, replica_groups=mesh['dp'=8,'tensor'=4] {'dp'}, dimensions={1} | all-to-all | bytes 14680064 | tf_op jit(solution)/shard_map/all_to_all | solution.py:19
  296.4 12.2 %all-gather.5.cloned.1.call-done = bf16[2048,3584]{1,0:T(8,128)(2,1)} async-done(((bf16[256,3584]{1,0:T(8,128)(2,1)}), bf16[2048,3584]{1,0:T(8,128)(2,1)}) %all-gather.5.cloned.1.call-update) | async-done | bytes 14680080 | tf_op jit(solution)/shard_map/all_gather | solution.py:22
  308.6 0.0 copy-start.1
  308.6 33.9 %convolution_multiply_fusion = f32[1792,3584]{1,0:T(8,128)} fusion(bf16[2048,1792]{1,0:T(8,128)(2,1)} %bitcast.13, bf16[2048,3584]{1,0:T(8,128)(2,1)} %all-gather.5.cloned.1.call-done), kind=kOutput, calls=%fused_computation | convolution fusion | flops 26313097216 | bytes 47710208 | tf_op jit(solution)/shard_map/dot_general | solution.py:20
  342.5 0.0 copy-done.1
Async XLA Ops:
  7.2 1.6 copy-start
  7.2 152.3 %all-gather.3.cloned.1.call-start = ((), (), s32[]{:S(2)}) async-start(), calls=%async_computation.1 | async-start | bytes 9175040 | tf_op jit(solution)/shard_map/all_gather | solution.py:18
  25.6 283.0 %all-gather.5.cloned.1.call-start = ((), (), s32[]{:S(2)}) async-start(), calls=%async_computation.2 | async-start | bytes 16515072 | tf_op jit(solution)/shard_map/all_gather | solution.py:22
  308.6 33.9 %copy-start.1 = (bf16[256,4096]{1,0:T(8,128)(2,1)S(1)}, bf16[256,4096]{1,0:T(8,128)(2,1)}, u32[]{:S(2)}) copy-start(bf16[256,4096]{1,0:T(8,128)(2,1)} %param.4) | copy-start | bytes 6291460
Sparse Core Ops, SparseCore 0:
  25.7 133.6 all-gather.2
  161.9 146.6 all-gather.4
where the time goes:
time: 352 us; the launch traced here: 349 us
  waiting for transfers between devices  146 us (41%)
  blocking collectives  133 us (38%)
  matrix products  50.7 us (14%)
  between operations  14.1 us (4%)
  local copies, waits for them, and re-layouts  5.11 us (1%)
    all_to_all x1, blocking collectives, local(): lax.all_to_all(all_columns_grad, 'dp', split_axis=1, concat_axis=0, tiled...  133 us
    all_gather x1, waiting for transfers between devices, local(): all_columns_grad = lax.all_gather(grad_gate, 'tensor', axis=1, tiled=True)  133 us
    dot_general x1, matrix products, local(): lax.dot_general(row_block, lax.all_gather(grad_gate, 'dp', axis=0, tiled=...  33.9 us
    dot_general x1, matrix products, local(): lax.dot_general(grad_out, down_weight, (((1,), (1,)), ((), ())), preferre...  16.8 us
    all_gather x1, waiting for transfers between devices, local(): lax.all_gather(grad_gate, 'dp', axis=0, tiled=True)  12.2 us
  transfers between devices with their start and end apart: 2, of which 2 were waited for; matrix products, arithmetic and copies ran while one was open for 1% of the time, Pallas kernels for 0%

commit v1 on v0

v1 whole, which is shorter than its diff:
```python
import functools

import jax
import jax.numpy as jnp
from jax import lax
from jax.experimental import pallas as pl
from jax.experimental.pallas import tpu as pltpu
from jax.sharding import PartitionSpec as P

MESH = pl.DeviceIdType.MESH
PIECES = 2


def both(*terms):
    out = terms[0]
    for term in terms[1:]:
        out = jnp.logical_and(out, term)
    return out


def gather_kernel(n, m, b_ref, buf, relay, local_sem, buf_sem, row_sem, relay_sem, send_sem):
    r = n // m
    tokens = b_ref.shape[1]
    piece = tokens // PIECES
    d, t = lax.axis_index("dp"), lax.axis_index("tensor")
    p, c = d // r, d % r
    last = m - 1
    sent = []

    def block(slot, source):
        return buf.at[slot, pl.ds(pl.multiple_of(source * tokens, tokens), tokens)]

    def part(slot, source, i):
        return buf.at[slot, pl.ds(pl.multiple_of(source * tokens + i * piece, piece), piece)]

    def send(when, src, dst, sem, dp, tensor):
        copy = pltpu.make_async_remote_copy(
            src_ref=src, dst_ref=dst, send_sem=send_sem.at[len(sent)], recv_sem=sem,
            device_id={"dp": dp, "tensor": tensor}, device_id_type=MESH,
        )
        sent.append((when, copy))

        @pl.when(when)
        def _():
            copy.start()

    def arrive(when, dst, sem):
        copy = pltpu.make_async_remote_copy(
            src_ref=dst, dst_ref=dst, send_sem=send_sem.at[0], recv_sem=sem,
            device_id={"dp": d, "tensor": t}, device_id_type=MESH,
        )

        @pl.when(when)
        def _():
            copy.wait_recv()

    here = d >= 0
    owner = p == t
    up, down = both(owner, t < last), both(owner, t > 0)
    lift, drop = both(p == last, t < last), both(p == 0, t > 0)

    def along_column(source, other, src_of):
        for i in range(PIECES):
            send(both(up, other != last), src_of(i), part(r, source, i), row_sem.at[source, i], d, t + 1)
            send(both(down, other != 0), src_of(i), part(r, source, i), row_sem.at[source, i], d, t - 1)

    for i in range(r):
        k = (c + i) % r
        send(lift, b_ref.at[k], relay.at[t, k], relay_sem.at[t, k], d, t + 1)
        send(drop, b_ref.at[k], relay.at[t, k], relay_sem.at[t, k], d, t - 1)
    along_column(d, p, lambda i: b_ref.at[c, pl.ds(i * piece, piece)])
    for i in range(1, r):
        c2 = (c + i) % r
        for k2 in range(r):
            k = (c2 + k2) % r
            send(here, b_ref.at[k], block(k, d), buf_sem.at[k, d], p * r + c2, t)
    xor = m & (m - 1) == 0
    tree = m == 4

    def partner(j):
        return p ^ j if xor else (p + j) % m

    def back(j):
        return p ^ j if xor else (p + m - j) % m

    for i in range(r):
        k = (c + i) % r
        for j in (1, 2) if tree else range(1, m):
            send(here, b_ref.at[k], block(k, d), buf_sem.at[k, d], partner(j) * r + k, t)
    own = pltpu.make_async_copy(b_ref, buf.at[pl.ds(0, r), pl.ds(pl.multiple_of(d * tokens, tokens), tokens)], local_sem)
    own.start()

    def share(source):
        for i in range(1, r):
            c2 = (c + i) % r
            send(here, block(c, source), block(c, source), buf_sem.at[c, source], p * r + c2, t)

    def column_event(j, e):
        other = back(j)
        source = other * r + (c + e) % r
        arrive(here, block(c, source), buf_sem.at[c, source])
        along_column(source, other, lambda i: part(c, source, i))
        if tree and j == 1:
            send(c % 2 == 0, block(c, source), block(c, source), buf_sem.at[c, source], (p ^ 2) * r + c, t)
        if tree and j == 2:
            send(c % 2 == 1, block(c, source), block(c, source), buf_sem.at[c, source], (p ^ 1) * r + c, t)
        share(source)

    def row_event(source, other):
        rise, fall = both(t > p, other != last), both(t < p, other != 0)
        for i in range(PIECES):
            at = part(r, source, i)
            arrive(jnp.logical_or(rise, fall), at, row_sem.at[source, i])
            send(both(rise, t < last), at, at, row_sem.at[source, i], d, t + 1)
            send(both(fall, t > 0), at, at, row_sem.at[source, i], d, t - 1)

    def relay_event(hops, e):
        for helper, step in ((last, -1), (0, 1)):
            origin = t + step * hops
            there = both(p == helper, origin >= 0, origin < m)
            slot = jnp.clip(origin, 0, last)
            k = (c + e) % r
            at = relay.at[slot, k]
            arrive(there, at, relay_sem.at[slot, k])
            send(both(there, t - step >= 0, t - step < m), at, at, relay_sem.at[slot, k], d, t - step)
            send(there, at, block(r, d), row_sem.at[d, 0], slot * r + k, t)

    def partner_event():
        for i in range(1, r):
            source = p * r + (c + i) % r
            arrive(here, block(c, source), buf_sem.at[c, source])
            along_column(source, p, lambda i: part(c, source, i))

    partner_event()
    row_event(d, p)
    column_event(1, 0)
    if m > 2:
        column_event(2, 0)
    relay_event(1, 0)
    for e in range(1, r):
        row_event(p * r + (c + e) % r, p)
        column_event(1, e)
        if m > 2:
            column_event(2, e)
        relay_event(1, e)
    for j in range(1, m):
        for e in range(r):
            if j + 2 < m:
                column_event(j + 2, e)
            other = back(j)
            row_event(other * r + (c + e) % r, other)
            if j + 1 < m:
                relay_event(j + 1, e)

    for e in range(r):
        for helper, when in ((last, t > p), (0, t < p)):
            source = helper * r + e
            arrive(when, block(r, source), row_sem.at[source, 0])
    for i in range(1, r):
        k = (c + i) % r
        for source in range(n):
            arrive(d != source, block(k, source), buf_sem.at[k, source])
    own.wait()
    for when, copy in sent:
        @pl.when(when)
        def _():
            copy.wait_send()


def gather(blocks, n, m):
    r, tokens, width = blocks.shape
    return pl.pallas_call(
        functools.partial(gather_kernel, n, m),
        out_shape=(
            jax.ShapeDtypeStruct((r + 1, n * tokens, width), blocks.dtype),
            jax.ShapeDtypeStruct((m, r, tokens, width), blocks.dtype),
        ),
        in_specs=[pl.BlockSpec(memory_space=pltpu.VMEM)],
        out_specs=(pl.BlockSpec(memory_space=pl.ANY), pl.BlockSpec(memory_space=pl.ANY)),
        scratch_shapes=[
            pltpu.SemaphoreType.DMA,
            pltpu.SemaphoreType.DMA((r, n)),
            pltpu.SemaphoreType.DMA((n, PIECES)),
            pltpu.SemaphoreType.DMA((m, r)),
            pltpu.SemaphoreType.DMA((SENDS[(n, m)],)),
        ],
        compiler_params=pltpu.CompilerParams(has_side_effects=True),
    )(blocks)


def gate_kernel(out_ref, weight_ref, gate_ref, up_ref, grad_gate_ref, grad_up_ref):
    hidden_grad = lax.dot_general(
        out_ref[...], weight_ref[...], (((1,), (1,)), ((), ())), preferred_element_type=jnp.float32
    )
    gate_value = gate_ref[...].astype(jnp.float32)
    sigmoid_gate = jax.nn.sigmoid(gate_value)
    silu_slope = sigmoid_gate * (1.0 + gate_value * (1.0 - sigmoid_gate))
    grad_gate_ref[0] = (hidden_grad * up_ref[...].astype(jnp.float32) * silu_slope).astype(jnp.bfloat16)
    grad_up_ref[...] = (hidden_grad * gate_value * sigmoid_gate).astype(jnp.bfloat16)


def tile_of(width, most):
    return max(size for size in range(128, most + 1, 128) if width % size == 0)


def gate(grad_out, down_weight, gate_pre, up_pre, r):
    tokens, depth = grad_out.shape
    columns = down_weight.shape[0]
    width = columns // r
    tile = tile_of(width, 256)
    per = width // tile
    flat = pl.BlockSpec((tokens, tile), lambda j: (0, j))
    return pl.pallas_call(
        gate_kernel,
        grid=(columns // tile,),
        out_shape=(
            jax.ShapeDtypeStruct((r, tokens, width), jnp.bfloat16),
            jax.ShapeDtypeStruct((tokens, columns), jnp.bfloat16),
        ),
        in_specs=[
            pl.BlockSpec((tokens, depth), lambda j: (0, 0)),
            pl.BlockSpec((tile, depth), lambda j: (j, 0)),
            flat,
            flat,
        ],
        out_specs=(pl.BlockSpec((1, tokens, tile), lambda j: (j // per, 0, j % per)), flat),
        compiler_params=pltpu.CompilerParams(vmem_limit_bytes=40 * 2**20),
    )(grad_out, down_weight, gate_pre, up_pre)


def factor_kernel(scale, slot_ref, rows_ref, columns_ref, out_ref):
    out_ref[...] = scale * lax.dot_general(
        rows_ref[0], columns_ref[0], (((0,), (0,)), ((), ())), preferred_element_type=jnp.float32
    )


def factor_of(buf, slot):
    r, total, width = buf.shape
    r -= 1
    tall, wide = tile_of(width, 256), tile_of(width, 896)
    per = width // wide
    return pl.pallas_call(
        functools.partial(factor_kernel, 1.0 / total),
        out_shape=jax.ShapeDtypeStruct((width, r * width), jnp.float32),
        grid_spec=pltpu.PrefetchScalarGridSpec(
            num_scalar_prefetch=1,
            grid=(r * per, width // tall),
            in_specs=[
                pl.BlockSpec((1, total, tall), lambda j, i, slot: (slot[0], 0, i)),
                pl.BlockSpec((1, total, wide), lambda j, i, slot: (j // per, 0, j % per)),
            ],
            out_specs=pl.BlockSpec((tall, wide), lambda j, i, slot: (i, j)),
        ),
        compiler_params=pltpu.CompilerParams(vmem_limit_bytes=40 * 2**20),
    )(slot, buf, buf)


def count(n, m):
    r = n // m
    tree = m == 4
    total = 2 * r + 2 * PIECES * r + (r - 1) * r + r * (2 if tree else m - 1)
    total += (m - 1) * r * (2 * PIECES + r - 1) + (2 * r if tree else 0)
    return total + n * PIECES * 2 + (m - 1) * r * 4


SENDS = {}


def solution(mesh):
    n, m = mesh.shape["dp"], mesh.shape["tensor"]
    assert n % m == 0 and m > 1
    r = n // m
    SENDS[(n, m)] = count(n, m)

    def local(grad_out, down_weight, gate_pre, up_pre):
        blocks, grad_up = gate(grad_out, down_weight, gate_pre, up_pre, r)
        buf, _ = gather(blocks, n, m)
        d, t = lax.axis_index("dp"), lax.axis_index("tensor")
        slot = jnp.where(d // r == t, d % r, r)
        factor = factor_of(buf, slot.astype(jnp.int32).reshape(1))
        return (factor, grad_up)

    return jax.shard_map(
        local,
        mesh=mesh,
        in_specs=(P("dp", None), P("tensor", None), P("dp", "tensor"), P("dp", "tensor")),
        out_specs=(P("dp", "tensor"), P("dp", "tensor")),
        check_vma=False,
    )
```

time: 352 us -> 247 us (0.70)
  Pallas kernels: 0 us -> 239 us
  waiting for transfers between devices: 146 us -> 0 us
  blocking collectives: 133 us -> 0 us
  matrix products: 50.7 us -> 0 us
  between operations: 14.1 us -> 0.67 us
    pallas_call x0 -> x3, Pallas kernels: none -> 239 us  [the longest x1 172 us: gather(): pl.pallas_call(functools.partial(gather_kernel, n, m), out_shape=(jax.Sha...]
    all_gather x2 -> x0, waiting for transfers between devices: 145 us -> none  [the longest x1 133 us: local(): all_columns_grad = lax.all_gather(grad_gate, 'tensor', axis=1, tiled=True)]
    all_to_all x1 -> x0, blocking collectives: 133 us -> none  [local(): lax.all_to_all(all_columns_grad, 'dp', split_axis=1, concat_axis=0, tiled...]
    dot_general x2 -> x0, matrix products: 50.7 us -> none  [the longest x1 33.9 us: local(): lax.dot_general(row_block, lax.all_gather(grad_gate, 'dp', axis=0, tiled=...]
    unnamed x4 -> x8, local copies, waits for them, and re-layouts: 1.55 us -> 5.81 us
    all_to_all x1 -> x0, local copies, waits for them, and re-layouts: 3.56 us -> none  [local(): lax.all_to_all(all_columns_grad, 'dp', split_axis=1, concat_axis=0, tiled...]
  transfers between devices with their start and end apart: 2 -> 0, of which waited for: 2 -> 0; matrix products, arithmetic and copies ran while one was open for 1% -> 0% of each run, Pallas kernels for 0% -> 0%
where the time goes in v1:
time: 247 us; the launch traced here: 246 us
  Pallas kernels  239 us (97%)
  local copies, waits for them, and re-layouts  5.81 us (2%)
    pallas_call x1, Pallas kernels, gather(): pl.pallas_call(functools.partial(gather_kernel, n, m), out_shape=(jax.Sha...  172 us
    pallas_call x1, Pallas kernels, factor_of(): pl.pallas_call(functools.partial(factor_kernel, 1.0 / total), out_shape=j...  47.9 us
    pallas_call x1, Pallas kernels, gate(): pl.pallas_call(gate_kernel, grid=(columns // tile,), out_shape=(jax.Shape...  19.3 us
    unnamed x8, local copies, waits for them, and re-layouts  5.81 us

profile of v1, /device:TPU:6, one launch (start us, length us, event | category | flops | bytes accessed | tf_op | source)
XLA Modules:
  0.0 245.8 jit_solution(7434148600435725717)
XLA Ops:
  0.7 0.0 copy-start
  0.7 1.6 copy-done
  2.2 0.0 copy-start.2
  2.2 1.5 copy-done.2
  3.7 0.0 copy-start.3
  3.7 1.5 copy-done.3
  5.2 19.3 %shard_map.59 = (bf16[2,256,1792]{2,1,0:T(8,128)(2,1)S(1)}, bf16[256,3584]{1,0:T(8,128)(2,1)}) custom-call(bf16[256,4096]{1,0:T(8,128)(2,1)S(1)} %copy-done, bf16[3584,4096]{1,0:T(8,128)(2,1)} %weight_ref.1, bf16[256,3584]{1,0:T(8,128)(2,1)S(1)} %copy-done.2, bf16[256,3584]{1,0:T(8,128)(2,1)S(1)} %copy-done.3), custom_call_target="tpu_custom_call" | custom-call | tf_op jit(solution)/shard_map/pallas_call | solution.py:213
  24.5 0.0 copy-start.1
  24.5 1.2 copy-done.1
  25.7 172.1 %shard_map.60 = (bf16[3,2048,1792]{2,1,0:T(8,128)(2,1)}, bf16[4,2,256,1792]{3,2,1,0:T(8,128)(2,1)}) custom-call(bf16[2,256,1792]{2,1,0:T(8,128)(2,1)} %copy-done.1), custom_call_target="tpu_custom_call" | custom-call | tf_op jit(solution)/shard_map/pallas_call | solution.py:172
  197.9 47.9 %shard_map.61 = f32[1792,3584]{1,0:T(8,128)} custom-call(s32[1]{0:T(128)} %bitcast.slot_ref, bf16[3,2048,1792]{2,1,0:T(8,128)(2,1)} %get-tuple-element.6.rows_ref.columns_ref, bf16[3,2048,1792]{2,1,0:T(8,128)(2,1)} %get-tuple-element.6.rows_ref.columns_ref), custom_call_target="tpu_custom_call" | custom-call | tf_op jit(solution)/shard_map/pallas_call | solution.py:242
Async XLA Ops:
  0.7 1.6 copy-start
  2.2 1.5 copy-start.2
  3.7 1.5 copy-start.3
  24.5 1.2 copy-start.1
